TPU v7x, 32 devices: a whole 2x2x4 slice. The times are simulated.
32 devices in a mesh: rep: 4 (over x, core), grp: 8 (over z, y).
Axes of the slice: x: 2, y: 2, z: 4, core: 2. Of those that a mesh axis runs over, the one named last changes fastest.
Arguments:
- tokens: bfloat16 [8192, 2304], P(('rep', 'grp')), may hold values from -6 to 6
- norm_gain: float32 [2304], replicated, may hold values from 0.25 to 1.75
- key_weight: bfloat16 [2304, 1024], P('grp'), may hold values from -0.125 to 0.125
- key_grad: bfloat16 [8192, 1024], P(('rep', 'grp')), may hold values from -6 to 6
Outputs:
- token_grad: bfloat16 [8192, 2304], P(('rep', 'grp'))
- weight_grad: float32 [2304, 1024], P('grp', 'rep')
- gain_grad: float32 [2304], replicated
All inputs are finite; a program needn't handle non-finite values.
Results may differ from a plain program's by a relative error of at most 0.023.
Values may be sent and summed in bfloat16 or wider, within the bound.
No kernel may reach another device: no remote copies, remote signals or barrier semaphores. Data moves between devices by JAX's collectives and lax.ppermute only.
A program may use at most 64 MiB of HBM per device.

v0:
```python
import jax
import jax.numpy as jnp
from jax import lax
from jax.sharding import PartitionSpec as P

epsilon = 1e-06


def shards(tokens, norm_gain, key_weight, key_grad):
    total_tokens = tokens.shape[0] * lax.axis_size("rep") * lax.axis_size("grp")
    grad_scale = total_tokens ** (-0.5)
    wide_tokens = tokens.astype(jnp.float32)
    inv_rms = lax.rsqrt(jnp.mean(wide_tokens * wide_tokens, axis=1, keepdims=True) + epsilon)
    normed = (wide_tokens * inv_rms * norm_gain).astype(jnp.bfloat16)
    partial_value = lax.dot_general(
        normed, key_grad, (((0,), (0,)), ((), ())), preferred_element_type=jnp.float32
    )
    d_normed = lax.dot_general(
        key_grad,
        lax.all_gather(key_weight, "grp", axis=0, tiled=True),
        (((1,), (1,)), ((), ())),
        preferred_element_type=jnp.float32,
    )
    section_one = lax.psum_scatter(
        partial_value.astype(jnp.bfloat16), "rep", scatter_dimension=1, tiled=True
    ).astype(jnp.float32)
    weight_sum = lax.psum_scatter(section_one, "grp", scatter_dimension=0, tiled=True)
    gain_local = jnp.sum(d_normed * wide_tokens * inv_rms, axis=0)
    gain_total = lax.psum(gain_local, ("rep", "grp"))
    scaled = d_normed * norm_gain
    inner_mean = jnp.mean(scaled * wide_tokens, axis=1, keepdims=True)
    token_grad = (inv_rms * (scaled - wide_tokens * inv_rms * inv_rms * inner_mean)).astype(
        jnp.bfloat16
    )
    return (token_grad, weight_sum * grad_scale, gain_total * grad_scale)


def solution(mesh):
    in_specs = (P(("rep", "grp"), None), P(), P("grp", None), P(("rep", "grp"), None))
    out_specs = (P(("rep", "grp"), None), P("grp", "rep"), P())
    return jax.shard_map(shards, mesh=mesh, in_specs=in_specs, out_specs=out_specs, check_vma=False)
```

profile of v0, /device:TPU:0, one launch (start us, length us, event | category | flops | bytes accessed | tf_op | source)
XLA Modules:
  0.0 180.5 jit_solution(7372656190298099384)
XLA Ops:
  8.0 0.0 copy-start
  8.0 0.0 reduce-scatter.3.cloned.1.call-start
  8.1 1.6 fusion.7
  9.7 0.0 copy-done
  9.7 5.0 %convolution_convert_fusion = bf16[2304,1024]{1,0:T(8,128)(2,1)} fusion(bf16[256,1024]{1,0:T(8,128)(2,1)S(1)} %copy-done, bf16[256,2304]{1,0:T(8,128)(2,1)} %param.4, f32[2304]{0:T(1024)} %param.5, f32[256]{0:T(256)S(1)} %add_rsqrt_fusion), kind=kOutput, calls=%fused_computation | convolution fusion | flops 1212678144 | bytes 6432768 | tf_op jit(solution)/shard_map/dot_general | solution.py:15
  14.7 0.0 reduce-scatter.3.cloned.1.call-update
  14.7 0.0 all-gather.2.cloned.1.call-start
  14.8 0.5 all-gather.2.cloned.1.call-update
  15.3 0.0 copy-start.1
  15.3 0.0 copy-start.2
  15.3 0.0 reduce-scatter.5.cloned.1.call-start
  15.4 50.0 %reduce-scatter.3.cloned.1.call-done = bf16[2304,256]{1,0:T(8,128)(2,1)} async-done(((bf16[2304,1024]{1,0:T(8,128)(2,1)}), bf16[2304,256]{1,0:T(8,128)(2,1)}) %reduce-scatter.3.cloned.1.call-update) | async-done | bytes 1179664 | tf_op jit(solution)/shard_map/reduce_scatter | solution.py:24
  65.3 2.9 %convert_element_type.19 = f32[2304,256]{1,0:T(8,128)} convert(bf16[2304,256]{1,0:T(8,128)(2,1)} %reduce-scatter.3.cloned.1.call-done) | non-fusion elementwise | flops 589824 | bytes 3538944 | tf_op jit(solution)/shard_map/convert_element_type | solution.py:26
  68.3 0.0 reduce-scatter.5.cloned.1.call-update
  68.3 30.9 %all-gather.2.cloned.1.call-done = bf16[2304,1024]{1,0:T(8,128)(2,1)} async-done(((bf16[288,1024]{1,0:T(8,128)(2,1)}), bf16[2304,1024]{1,0:T(8,128)(2,1)}) %all-gather.2.cloned.1.call-update) | async-done | bytes 4718608 | tf_op jit(solution)/shard_map/all_gather | solution.py:20
  99.2 0.0 copy-done.1
  99.2 0.0 copy-done.2
  99.2 5.6 %fusion.10 = (f32[2304]{0:T(1024)S(1)}, f32[256]{0:T(256)S(1)}, f32[256,2304]{1,0:T(8,128)}) fusion(bf16[256,2304]{1,0:T(8,128)(2,1)S(1)} %copy-done.1, f32[256]{0:T(256)S(1)} %add_rsqrt_fusion, f32[2304]{0:T(1024)S(1)} %copy-done.2, bf16[256,1024]{1,0:T(8,128)(2,1)S(1)} %copy-done, bf16[2304,1024]{1,0:T(8,128)(2,1)} %all-gather.2.cloned.1.call-done), kind=kOutput, calls=%fused_computation.15 | convolution fusion | flops 1212085760 | bytes 8802304 | tf_op jit(solution)/shard_map/dot_general | solution.py:18
  104.8 39.4 %psum.7 = f32[2304]{0:T(1024)S(1)} all-reduce(f32[2304]{0:T(1024)S(1)} %get-tuple-element.3), channel_id=1, replica_groups=mesh['rep'=4,'grp'=8] {'rep','grp'}, use_global_device_ids=true, to_apply=%region_5.0 | all-reduce | flops 2304 | bytes 18432 | tf_op jit(solution)/shard_map/psum | solution.py:29
  144.2 0.6 broadcast_multiply_fusion.1
  144.8 3.4 %fusion.5 = bf16[256,2304]{1,0:T(8,128)(2,1)} fusion(bf16[256,2304]{1,0:T(8,128)(2,1)S(1)} %copy-done.1, f32[256,2304]{1,0:T(8,128)} %get-tuple-element.5, f32[256]{0:T(256)S(1)} %broadcast_multiply_fusion.2, f32[2304]{0:T(1024)S(1)} %copy-done.2, f32[256]{0:T(256)S(1)} %add_rsqrt_fusion), kind=kLoop, calls=%fused_computation.10 | loop fusion | flops 4718592 | bytes 4729856 | tf_op jit(solution)/shard_map/convert_element_type | solution.py:32
  148.2 23.2 %reduce-scatter.5.cloned.1.call-done = f32[288,256]{1,0:T(8,128)} async-done(((f32[2304,256]{1,0:T(8,128)}), f32[288,256]{1,0:T(8,128)}) %reduce-scatter.5.cloned.1.call-update) | async-done | bytes 294928 | tf_op jit(solution)/shard_map/reduce_scatter | solution.py:27
  171.4 1.7 broadcast_multiply_fusion
  (2 shorter events, 0.0 us)
Async XLA Ops:
  8.0 1.7 copy-start
  8.0 57.3 %reduce-scatter.3.cloned.1.call-start = ((), (), s32[]{:S(2)}) async-start(), calls=%async_computation.3 | async-start | bytes 5898240 | tf_op jit(solution)/shard_map/reduce_scatter | solution.py:24
  14.7 84.5 %all-gather.2.cloned.1.call-start = ((), (), s32[]{:S(2)}) async-start(), calls=%async_computation.2 | async-start | bytes 5308416 | tf_op jit(solution)/shard_map/all_gather | solution.py:20
  15.3 83.9 %copy-start.1 = (bf16[256,2304]{1,0:T(8,128)(2,1)S(1)}, bf16[256,2304]{1,0:T(8,128)(2,1)}, u32[]{:S(2)}) copy-start(bf16[256,2304]{1,0:T(8,128)(2,1)} %param.4) | copy-start | bytes 3538948
  15.3 83.9 %copy-start.2 = (f32[2304]{0:T(1024)S(1)}, f32[2304]{0:T(1024)}, u32[]{:S(2)}) copy-start(f32[2304]{0:T(1024)} %param.5) | copy-start | bytes 27652
  15.3 156.1 %reduce-scatter.5.cloned.1.call-start = ((), (), s32[]{:S(2)}) async-start(), calls=%async_computation.4 | async-start | bytes 2654208 | tf_op jit(solution)/shard_map/reduce_scatter | solution.py:27
Sparse Core Ops, SparseCore 0:
  14.8 50.4 reduce-scatter.2
Sparse Core Ops, SparseCore 1:
  17.4 81.8 all-gather.1
  102.6 68.8 reduce-scatter.4
where the time goes:
time: 181 us
  waiting for transfers between devices  105 us (58%)
  blocking collectives  39.4 us (22%)
  between operations  15.5 us (9%)
  matrix products  10.6 us (6%)
  other arithmetic  10.2 us (6%)
    reduce_scatter x1, waiting for transfers between devices, shards(): lax.psum_scatter(partial_value.astype(jnp.bfloat16), 'rep', scatter_dimen...  50 us
    psum x1, blocking collectives, shards(): gain_total = lax.psum(gain_local, ('rep', 'grp'))  39.4 us
    all_gather x1, waiting for transfers between devices, shards(): lax.all_gather(key_weight, 'grp', axis=0, tiled=True)  30.9 us
    reduce_scatter x1, waiting for transfers between devices, shards(): lax.psum_scatter(section_one, 'grp', scatter_dimension=0, tiled=True)  23.2 us
    dot_general x1, matrix products, shards(): lax.dot_general(key_grad, lax.all_gather(key_weight, 'grp', axis=0, tiled...  5.59 us
    dot_general x1, matrix products, shards(): lax.dot_general(normed, key_grad, (((0,), (0,)), ((), ())), preferred_ele...  4.97 us
  transfers between devices with their start and end apart: 3, of which 3 were waited for; matrix products, arithmetic and copies ran while one was open for 7% of the time, Pallas kernels for 0%

commit v1 on v0

--- a/solution.py
+++ b/solution.py
@@ -26,7 +26,7 @@
     ).astype(jnp.float32)
     weight_sum = lax.psum_scatter(section_one, "grp", scatter_dimension=0, tiled=True)
     gain_local = jnp.sum(d_normed * wide_tokens * inv_rms, axis=0)
-    gain_total = lax.psum(gain_local, ("rep", "grp"))
+    gain_total = jnp.sum(lax.all_gather(gain_local, ("rep", "grp")), axis=0)
     scaled = d_normed * norm_gain
     inner_mean = jnp.mean(scaled * wide_tokens, axis=1, keepdims=True)
     token_grad = (inv_rms * (scaled - wide_tokens * inv_rms * inv_rms * inner_mean)).astype(

time: 181 us -> 187 us (1.033)
  blocking collectives: 39.4 us -> 68.2 us
  waiting for transfers between devices: 105 us -> 81.5 us
    all_gather x0 -> x1, blocking collectives: none -> 68.2 us  [shards(): gain_total = jnp.sum(lax.all_gather(gain_local, ('rep', 'grp')), axis=0)]
    psum x1 -> x0, blocking collectives: 39.4 us -> none  [shards(): gain_total = lax.psum(gain_local, ('rep', 'grp'))]
    reduce_scatter x1, waiting for transfers between devices: 23.2 us -> 0.01 us  [shards(): lax.psum_scatter(section_one, 'grp', scatter_dimension=0, tiled=True)]
  transfers between devices with their start and end apart: 3 -> 3, of which waited for: 3 -> 2; matrix products, arithmetic and copies ran while one was open for 7% -> 7% of each run, Pallas kernels for 0% -> 0%
where the time goes in v1:
time: 187 us; the launch traced here: 186 us
  waiting for transfers between devices  81.5 us (44%)
  blocking collectives  68.2 us (36%)
  between operations  15.5 us (8%)
  matrix products  10.6 us (6%)
  other arithmetic  10.4 us (6%)
    all_gather x1, blocking collectives, shards(): gain_total = jnp.sum(lax.all_gather(gain_local, ('rep', 'grp')), axis=0)  68.2 us
    reduce_scatter x1, waiting for transfers between devices, shards(): lax.psum_scatter(partial_value.astype(jnp.bfloat16), 'rep', scatter_dimen...  50 us
    all_gather x1, waiting for transfers between devices, shards(): lax.all_gather(key_weight, 'grp', axis=0, tiled=True)  30.9 us
    dot_general x1, matrix products, shards(): lax.dot_general(key_grad, lax.all_gather(key_weight, 'grp', axis=0, tiled...  5.59 us
    dot_general x1, matrix products, shards(): lax.dot_general(normed, key_grad, (((0,), (0,)), ((), ())), preferred_ele...  4.97 us
  transfers between devices with their start and end apart: 3, of which 2 were waited for; matrix products, arithmetic and copies ran while one was open for 7% of the time, Pallas kernels for 0%

profile of v1, /device:TPU:0, one launch (start us, length us, event | category | flops | bytes accessed | tf_op | source)
XLA Modules:
  0.0 186.3 jit_solution(14885376129136466503)
XLA Ops:
  8.0 0.0 copy-start
  8.0 0.0 reduce-scatter.3.cloned.1.call-start
  8.1 1.6 fusion.7
  9.7 0.0 copy-done
  9.7 5.0 %convolution_convert_fusion = bf16[2304,1024]{1,0:T(8,128)(2,1)} fusion(bf16[256,1024]{1,0:T(8,128)(2,1)S(1)} %copy-done, bf16[256,2304]{1,0:T(8,128)(2,1)} %param.4, f32[2304]{0:T(1024)} %param.5, f32[256]{0:T(256)S(1)} %add_rsqrt_fusion), kind=kOutput, calls=%fused_computation | convolution fusion | flops 1212678144 | bytes 6432768 | tf_op jit(solution)/shard_map/dot_general | solution.py:15
  14.7 0.0 reduce-scatter.3.cloned.1.call-update
  14.7 0.0 all-gather.4.cloned.1.call-start
  14.8 0.5 all-gather.4.cloned.1.call-update
  15.3 0.0 copy-start.1
  15.3 0.0 copy-start.2
  15.3 0.0 reduce-scatter.5.cloned.1.call-start
  15.4 50.0 %reduce-scatter.3.cloned.1.call-done = bf16[2304,256]{1,0:T(8,128)(2,1)} async-done(((bf16[2304,1024]{1,0:T(8,128)(2,1)}), bf16[2304,256]{1,0:T(8,128)(2,1)}) %reduce-scatter.3.cloned.1.call-update) | async-done | bytes 1179664 | tf_op jit(solution)/shard_map/reduce_scatter | solution.py:24
  65.3 2.9 %convert_element_type.19 = f32[2304,256]{1,0:T(8,128)} convert(bf16[2304,256]{1,0:T(8,128)(2,1)} %reduce-scatter.3.cloned.1.call-done) | non-fusion elementwise | flops 589824 | bytes 3538944 | tf_op jit(solution)/shard_map/convert_element_type | solution.py:26
  68.3 0.0 reduce-scatter.5.cloned.1.call-update
  68.3 30.9 %all-gather.4.cloned.1.call-done = bf16[2304,1024]{1,0:T(8,128)(2,1)} async-done(((bf16[288,1024]{1,0:T(8,128)(2,1)}), bf16[2304,1024]{1,0:T(8,128)(2,1)}) %all-gather.4.cloned.1.call-update) | async-done | bytes 4718608 | tf_op jit(solution)/shard_map/all_gather | solution.py:20
  99.2 0.0 copy-done.1
  99.2 0.0 copy-done.2
  99.2 5.6 %fusion.10 = (f32[2304]{0:T(1024)S(1)}, f32[256]{0:T(256)S(1)}, f32[256,2304]{1,0:T(8,128)}) fusion(bf16[256,2304]{1,0:T(8,128)(2,1)S(1)} %copy-done.1, f32[256]{0:T(256)S(1)} %add_rsqrt_fusion, f32[2304]{0:T(1024)S(1)} %copy-done.2, bf16[256,1024]{1,0:T(8,128)(2,1)S(1)} %copy-done, bf16[2304,1024]{1,0:T(8,128)(2,1)} %all-gather.4.cloned.1.call-done), kind=kOutput, calls=%fused_computation.15 | convolution fusion | flops 1212085760 | bytes 8802304 | tf_op jit(solution)/shard_map/dot_general | solution.py:18
  104.8 68.2 %all-gather.1 = f32[32,1,2304]{2,1,0:T(1,128)S(1)} all-gather(f32[1,1,2304]{2,1,0:T(1,128)S(1)} %reshape.20), channel_id=2, replica_groups=mesh['rep'=4,'grp'=8] {'rep','grp'}, dimensions={0}, use_global_device_ids=true | all-gather | bytes 304128 | tf_op jit(solution)/shard_map/all_gather | solution.py:29
  173.0 0.2 reduce_sum.39
  173.2 0.6 broadcast_multiply_fusion.1
  173.8 3.4 %fusion.5 = bf16[256,2304]{1,0:T(8,128)(2,1)} fusion(bf16[256,2304]{1,0:T(8,128)(2,1)S(1)} %copy-done.1, f32[256,2304]{1,0:T(8,128)} %get-tuple-element.5, f32[256]{0:T(256)S(1)} %broadcast_multiply_fusion.2, f32[2304]{0:T(1024)S(1)} %copy-done.2, f32[256]{0:T(256)S(1)} %add_rsqrt_fusion), kind=kLoop, calls=%fused_computation.10 | loop fusion | flops 4718592 | bytes 4729856 | tf_op jit(solution)/shard_map/convert_element_type | solution.py:32
  177.2 0.0 reduce-scatter.5.cloned.1.call-done
  177.2 1.7 broadcast_multiply_fusion
  (3 shorter events, 0.0 us)
Async XLA Ops:
  8.0 1.7 copy-start
  8.0 57.3 %reduce-scatter.3.cloned.1.call-start = ((), (), s32[]{:S(2)}) async-start(), calls=%async_computation.3 | async-start | bytes 5898240 | tf_op jit(solution)/shard_map/reduce_scatter | solution.py:24
  14.7 84.5 %all-gather.4.cloned.1.call-start = ((), (), s32[]{:S(2)}) async-start(), calls=%async_computation.2 | async-start | bytes 5308416 | tf_op jit(solution)/shard_map/all_gather | solution.py:20
  15.3 83.9 %copy-start.1 = (bf16[256,2304]{1,0:T(8,128)(2,1)S(1)}, bf16[256,2304]{1,0:T(8,128)(2,1)}, u32[]{:S(2)}) copy-start(bf16[256,2304]{1,0:T(8,128)(2,1)} %param.4) | copy-start | bytes 3538948
  15.3 83.9 %copy-start.2 = (f32[2304]{0:T(1024)S(1)}, f32[2304]{0:T(1024)}, u32[]{:S(2)}) copy-start(f32[2304]{0:T(1024)} %param.5) | copy-start | bytes 27652
  15.3 161.9 %reduce-scatter.5.cloned.1.call-start = ((), (), s32[]{:S(2)}) async-start(), calls=%async_computation.4 | async-start | bytes 2654208 | tf_op jit(solution)/shard_map/reduce_scatter | solution.py:27
Sparse Core Ops, SparseCore 0:
  14.8 50.4 reduce-scatter.2
Sparse Core Ops, SparseCore 1:
  17.4 81.8 all-gather.3
  102.6 69.1 reduce-scatter.4
